TPU v7x, 32 devices: a whole 2x2x4 slice. The times are simulated.
32 devices in a mesh: gx: 16 (over z, y, x), gy: 2 (over core).
Axes of the slice: x: 2, y: 2, z: 4, core: 2. Of those that a mesh axis runs over, the one named last changes fastest.
Arguments:
- residual: bfloat16 [16, 2, 2048, 384], P('gx', 'gy'), may hold values from -6 to 6
- local_inverse: bfloat16 [16, 2, 2048, 2048], P('gx', 'gy'), may hold values from -0.125 to 0.125
- primal_basis: bfloat16 [16, 2, 96, 2048], P('gx', 'gy'), may hold values from -0.125 to 0.125
- row_stiffness: bfloat16 [16, 2, 2048], P('gx', 'gy'), may hold values from 0.099609375 to 10
- face_sizes: int32 [16, 2, 4], P('gx', 'gy'), may hold values from 0 to 512, as said below
- primal_slots: int32 [16, 2, 96], P('gx', 'gy'), may hold values from 0 to 287
- block_inverse: float32 [16, 2, 32, 64], P('gx', 'gy'), may hold values from -1 to 3
- level_basis: float32 [16, 2, 32, 64], P('gx', 'gy'), may hold values from -0.15625 to 0.15625
- top_inverse: float32 [64, 64], replicated, may hold values from -1 to 3
Outputs:
- preconditioned: bfloat16 [16, 2, 2048, 384], P('gx', 'gy')
Inputs may be any that keep to these rules, and one draw needn't show every extreme that they name: face_sizes[x, y, f] is equal on the two sides of a shared face, 0 on faces at the grid's edge, at least 128 elsewhere; the value 512 is reached.
All inputs are finite; a program needn't handle non-finite values.
Results may differ from a plain program's by a relative error of at most 0.008.
Values may be sent and summed in bfloat16 or wider, within the bound.
No kernel may reach another device: no remote copies, remote signals or barrier semaphores. Data moves between devices by JAX's collectives and lax.ppermute only.
A program may use at most 64 MiB of HBM per device.

v0:
```python
import jax
import jax.numpy as jnp
from jax import lax
from jax.sharding import PartitionSpec as P


def passed_along(block, axis, distance):
    devices = range(lax.axis_size(axis))
    route = [(i - distance, i) for i in devices if i - distance in devices]
    return lax.ppermute(block, axis, route)


def extended(block, sides, width):
    for axis, dim in sides:
        count = lax.axis_size(axis)
        forward = [(i, i + 1) for i in range(count - 1)]
        backward = [(target, source) for source, target in forward]
        low = lax.ppermute(
            lax.slice_in_dim(block, block.shape[dim] - width, None, axis=dim), axis, forward
        )
        high = lax.ppermute(lax.slice_in_dim(block, 0, width, axis=dim), axis, backward)
        block = jnp.concatenate([low, block, high], axis=dim)
    return block


def coarse_lift(phi_block, values, stiffness_block):
    coarse_rows = jnp.einsum("pw,pr->wr", phi_block, values, precision=lax.Precision.HIGHEST)
    return stiffness_block[:, None] * coarse_rows


def local(
    residual,
    local_inverse,
    primal_basis,
    row_stiffness,
    face_sizes,
    primal_slots,
    block_inverse,
    level_basis,
    top_inverse,
):
    highest = lax.Precision.HIGHEST
    own_rows = residual[0, 0]
    row_count = own_rows.shape[0]
    face_rows = row_count // 4
    coarse_count = block_inverse.shape[2]
    counts = face_sizes[0, 0]
    position = jnp.arange(row_count, dtype=jnp.int32)
    face_of_row = position // face_rows
    picked = jnp.where(
        face_of_row[:, None] == jnp.arange(4, dtype=jnp.int32)[None, :], counts[None, :], 0
    )
    live_rows = position % face_rows < jnp.sum(picked, axis=1)
    masked = jnp.where(live_rows[:, None], own_rows, jnp.zeros((), jnp.bfloat16))
    local_part = jnp.dot(local_inverse[0, 0], masked, preferred_element_type=jnp.float32)
    primal_phi = primal_basis[0, 0]
    partial_value = jnp.dot(primal_phi, masked, preferred_element_type=jnp.float32)
    selector = (
        primal_slots[0, 0][:, None] == jnp.arange(9 * coarse_count, dtype=jnp.int32)[None, :]
    ).astype(jnp.float32)
    spread = jnp.einsum("ps,pr->sr", selector, partial_value, precision=highest).reshape(
        3, 3, coarse_count, -1
    )
    from_below_y = passed_along(spread[:, 2], "gy", 1)
    from_above_y = passed_along(spread[:, 0], "gy", -1)
    along_x = spread[:, 1] + from_below_y + from_above_y
    from_below_x = passed_along(along_x[2], "gx", 1)
    from_above_x = passed_along(along_x[0], "gx", -1)
    assembled = along_x[1] + from_below_x + from_above_x
    level_phi = level_basis[0, 0]
    top_rhs = lax.psum(
        jnp.einsum("cl,cr->lr", level_phi, assembled, precision=highest), ("gx", "gy")
    )
    top_value = jnp.dot(top_inverse, top_rhs, precision=highest)
    block_rhs = lax.all_gather(assembled, "gy", axis=0, tiled=True)
    coarse = jnp.dot(block_inverse[0, 0], block_rhs, precision=highest) + jnp.dot(
        level_phi, top_value, precision=highest
    )
    beside_all = extended(coarse[None, None], (("gx", 0), ("gy", 1)), 1)
    primal_values = jnp.dot(selector, beside_all.reshape(9 * coarse_count, -1), precision=highest)
    stiffness = row_stiffness[0, 0]
    stiffness_f = stiffness.astype(jnp.float32)
    phi_f = primal_phi.astype(jnp.float32)
    local_weighted = jnp.where(live_rows[:, None], stiffness_f[:, None] * local_part, 0.0)
    own_total = local_weighted + coarse_lift(phi_f, primal_values, stiffness_f)
    sent = jnp.where(live_rows[:, None], own_total, 0.0).astype(jnp.bfloat16)

    def face_parts(values):
        return [values[face_id * face_rows : (face_id + 1) * face_rows] for face_id in range(4)]

    stiff_faces = face_parts(stiffness)
    sent_faces = face_parts(sent)
    recv_low_x = passed_along((sent_faces[1], stiff_faces[1]), "gx", 1)
    recv_high_x = passed_along((sent_faces[0], stiff_faces[0]), "gx", -1)
    recv_low_y = passed_along((sent_faces[3], stiff_faces[3]), "gy", 1)
    recv_high_y = passed_along((sent_faces[2], stiff_faces[2]), "gy", -1)
    received = [recv_low_x, recv_high_x, recv_low_y, recv_high_y]
    other_sent = jnp.concatenate([item[0] for item in received], axis=0)
    other_stiffness = jnp.concatenate([item[1] for item in received], axis=0)
    summed = sent.astype(jnp.float32) + other_sent.astype(jnp.float32)
    divisor = stiffness_f + other_stiffness.astype(jnp.float32)
    result = jnp.where(live_rows[:, None], summed / divisor[:, None], 0.0).astype(jnp.bfloat16)
    return result[None, None]


def solution(mesh):
    in_specs = (
        P("gx", "gy", None, None),
        P("gx", "gy", None, None),
        P("gx", "gy", None, None),
        P("gx", "gy", None),
        P("gx", "gy", None),
        P("gx", "gy", None),
        P("gx", "gy", None, None),
        P("gx", "gy", None, None),
        P(),
    )
    out_specs = P("gx", "gy", None, None)
    return jax.shard_map(local, mesh=mesh, in_specs=in_specs, out_specs=out_specs, check_vma=False)
```

profile of v0, /device:TPU:7, one launch (start us, length us, event | category | flops | bytes accessed | tf_op | source)
XLA Modules:
  0.0 229.3 jit_solution(7290555290257131025)
XLA Ops:
  6.5 0.0 copy-start
  6.5 0.0 copy-start.5
  6.5 0.0 copy-start.1
  6.5 0.0 all-reduce.2.cloned.1.call-start
  6.6 0.8 select_reduce_fusion
  7.4 0.2 copy-done
  7.5 0.0 copy-start.3
  7.5 0.0 copy-start.4
  7.6 0.0 copy-start.2
  7.6 2.4 %fusion.7 = f32[384,96]{1,0:T(8,128)S(1)} fusion(bf16[1,1,2048,384]{3,2,1,0:T(8,128)(2,1)} %param.9, pred[2048]{0:T(1024)(128)(4,1)S(1)} %fusion.29, bf16[1,1,96,2048]{3,2,1,0:T(8,128)(2,1)S(1)} %copy-done), kind=kOutput, calls=%fused_computation.5 | convolution fusion | flops 151781376 | bytes 2115584 | tf_op jit(solution)/shard_map/dot_general | solution.py:57
  10.0 0.0 copy-done.5
  10.0 0.5 fusion.19
  10.5 1.3 collective-permute-start
  11.8 3.0 %collective-permute-start.1 = (f32[3,32,384]{2,1,0:T(8,128)S(1)}, f32[3,32,384]{2,1,0:T(8,128)S(1)}, u32[]{:S(2)}, u32[]{:S(2)}) collective-permute-start(f32[3,32,384]{2,1,0:T(8,128)S(1)} %get-tuple-element.14), channel_id=1, source_target_pairs={{1,0},{3,2},{5,4},{7,6},{9,8},{11,10},{13,12},{15,14},{17,16},{19,... | collective-permute-start | bytes 442376 | tf_op jit(solution)/shard_map/ppermute | solution.py:10
  14.8 0.0 collective-permute-done
  14.8 1.0 collective-permute-done.1
  15.8 3.1 %collective-permute-start.2 = (f32[32,384]{1,0:T(8,128)S(1)}, f32[32,384]{1,0:T(8,128)S(1)}, u32[]{:S(2)}, u32[]{:S(2)}) collective-permute-start(f32[32,384]{1,0:T(8,128)S(1)} %get-tuple-element.15), channel_id=1, source_target_pairs={{0,2},{2,4},{4,6},{6,8},{8,10},{10,12},{12,14},{14,16},{16,18},{18... | collective-permute-start | bytes 147464 | tf_op jit(solution)/shard_map/ppermute | solution.py:10
  19.0 2.2 collective-permute-start.3
  21.1 0.0 collective-permute-done.2
  21.1 4.5 %collective-permute-done.3 = f32[32,384]{1,0:T(8,128)S(1)} collective-permute-done((f32[32,384]{1,0:T(8,128)S(1)}, f32[32,384]{1,0:T(8,128)S(1)}, u32[]{:S(2)}, u32[]{:S(2)}) %collective-permute-start.3) | collective-permute-done | bytes 49184 | tf_op jit(solution)/shard_map/ppermute | solution.py:10
  25.6 0.0 copy-done.1
  25.6 1.2 convolution_bitcast_fusion
  26.8 0.0 all-reduce.2.cloned.1.call-update
  26.8 3.3 %all_gather.3 = f32[64,384]{1,0:T(8,128)S(1)} all-gather(f32[32,384]{1,0:T(8,128)S(1)} %fusion.24), channel_id=1, replica_groups=mesh['gx'=16,'gy'=2] {'gy'}, dimensions={0}, use_global_device_ids=true | all-gather | bytes 147456 | tf_op jit(solution)/shard_map/all_gather | solution.py:75
  30.1 0.0 copy-start.6
  30.1 121.2 %all-reduce.2.cloned.1.call-done = f32[64,384]{0,1:T(8,128)} async-done(((f32[64,384]{0,1:T(8,128)}), f32[64,384]{0,1:T(8,128)}) %all-reduce.2.cloned.1.call-update) | async-done | bytes 98320 | tf_op jit(solution)/shard_map/psum | solution.py:71
  151.4 0.0 copy-done.3
  151.4 1.2 fusion.38
  152.6 0.3 fusion.25
  153.0 0.0 copy-done.4
  153.0 0.2 fusion.11
  153.2 4.6 %collective-permute-start.4 = (f32[1,1,32,384]{3,2,1,0:T(8,128)S(1)}, f32[1,1,32,384]{3,2,1,0:T(8,128)S(1)}, u32[]{:S(2)}, u32[]{:S(2)}) collective-permute-start(f32[1,1,32,384]{3,2,1,0:T(8,128)S(1)} %fusion.11), channel_id=1, source_target_pairs={{0,2},{2,4},{4,6},{6,8},{8,10},{10,12},{12,14},{14,16},{16,18},{18... | collective-permute-start | bytes 147464 | tf_op jit(solution)/shard_map/ppermute | solution.py:18
  157.8 1.9 collective-permute-start.5
  159.7 0.0 collective-permute-done.4
  159.7 4.7 %collective-permute-done.5 = f32[1,1,32,384]{3,2,1,0:T(8,128)S(1)} collective-permute-done((f32[1,1,32,384]{3,2,1,0:T(8,128)S(1)}, f32[1,1,32,384]{3,2,1,0:T(8,128)S(1)}, u32[]{:S(2)}, u32[]{:S(2)}) %collective-permute-start.5) | collective-permute-done | bytes 49184 | tf_op jit(solution)/shard_map/ppermute | solution.py:21
  164.5 1.3 collective-permute-start.6
  165.8 5.9 %collective-permute-start.7 = (f32[3,1,32,384]{3,2,1,0:T(8,128)S(1)}, f32[3,1,32,384]{3,2,1,0:T(8,128)S(1)}, u32[]{:S(2)}, u32[]{:S(2)}) collective-permute-start(f32[3,1,32,384]{3,2,1,0:T(8,128)S(1)} %pad_maximum_fusion.1), channel_id=1, source_target_pairs={{1,0},{3,2},{5,4},{7,6},{9,8},{11,10},{13,12},{15,14},{17,16},{19,... | collective-permute-start | bytes 442376 | tf_op jit(solution)/shard_map/ppermute | solution.py:21
  171.7 0.0 copy-done.2
  171.7 0.0 collective-permute-done.6
  171.7 0.9 collective-permute-done.7
  172.7 0.4 fusion.17
  173.1 1.4 fusion.12
  174.5 0.0 copy-done.6
  174.6 7.5 %fusion.4 = bf16[2048,384]{0,1:T(8,128)(2,1)S(1)} fusion(f32[384,2048]{1,0:T(8,128)S(1)} %fusion.12, bf16[1,1,2048,2048]{3,2,1,0:T(8,128)(2,1)} %param.10, f32[2048]{0:T(1024)S(1)} %bitcast.75, pred[2048]{0:T(1024)(128)(4,1)S(1)} %fusion.29, bf16[1,1,2048,384]{3,2,1,0:T(8,128)(2,1)S(1)} %copy-done.6), kind=kOutput, calls=%fused_computation.4 | convolution fusion | flops 3226730496 | bytes 14690304 | tf_op jit(solution)/shard_map/dot_general | solution.py:55
  182.1 0.1 fusion.37
  182.2 1.3 collective-permute-start.10
  183.5 3.1 %collective-permute-start.11 = (bf16[512,384]{0,1:T(8,128)(2,1)S(1)}, bf16[512,384]{0,1:T(8,128)(2,1)S(1)}, u32[]{:S(2)}, u32[]{:S(2)}) collective-permute-start(bf16[512,384]{0,1:T(8,128)(2,1)S(1)} %get-tuple-element.10), channel_id=1, source_target_pairs={{1,0},{3,2},{5,4},{7,6},{9,8},{11,10},{13,12},{15,14},{17,16},{19,... | collective-permute-start | bytes 1179656 | tf_op jit(solution)/shard_map/ppermute | solution.py:10
  186.6 1.9 collective-permute-start.8
  188.5 3.4 %collective-permute-start.9 = (bf16[512,384]{0,1:T(8,128)(2,1)S(1)}, bf16[512,384]{0,1:T(8,128)(2,1)S(1)}, u32[]{:S(2)}, u32[]{:S(2)}) collective-permute-start(bf16[512,384]{0,1:T(8,128)(2,1)S(1)} %get-tuple-element.12), channel_id=1, source_target_pairs={{2,0},{4,2},{6,4},{8,6},{10,8},{12,10},{14,12},{16,14},{18,16},{20... | collective-permute-start | bytes 1179656 | tf_op jit(solution)/shard_map/ppermute | solution.py:10
  191.9 3.7 %collective-permute-start.12 = (bf16[512]{0:T(512)(128)(2,1)S(1)}, bf16[512]{0:T(512)(128)(2,1)S(1)}, u32[]{:S(2)}, u32[]{:S(2)}) collective-permute-start(bf16[512]{0:T(512)(128)(2,1)S(1)} %get-tuple-element.5), channel_id=1, source_target_pairs={{0,2},{2,4},{4,6},{6,8},{8,10},{10,12},{12,14},{14,16},{16,18},{18... | collective-permute-start | bytes 3080 | tf_op jit(solution)/shard_map/ppermute | solution.py:10
  195.6 12.1 %collective-permute-done.12 = bf16[512]{0:T(512)(128)(2,1)S(1)} collective-permute-done((bf16[512]{0:T(512)(128)(2,1)S(1)}, bf16[512]{0:T(512)(128)(2,1)S(1)}, u32[]{:S(2)}, u32[]{:S(2)}) %collective-permute-start.12) | collective-permute-done | bytes 1056 | tf_op jit(solution)/shard_map/ppermute | solution.py:10
  207.7 1.9 collective-permute-start.13
  209.6 4.2 %collective-permute-done.13 = bf16[512]{0:T(512)(128)(2,1)S(1)} collective-permute-done((bf16[512]{0:T(512)(128)(2,1)S(1)}, bf16[512]{0:T(512)(128)(2,1)S(1)}, u32[]{:S(2)}, u32[]{:S(2)}) %collective-permute-start.13) | collective-permute-done | bytes 1056 | tf_op jit(solution)/shard_map/ppermute | solution.py:10
  213.8 1.3 collective-permute-start.14
  215.1 2.2 collective-permute-done.14
  217.3 2.1 collective-permute-start.15
  219.3 0.8 collective-permute-done.15
  220.2 0.0 collective-permute-done.10
  220.2 0.0 collective-permute-done.11
  220.2 0.0 collective-permute-done.8
  220.2 0.0 collective-permute-done.9
  220.2 0.6 fusion.10
  220.8 1.6 copy.15
  (11 shorter events, 0.2 us)
Async XLA Ops:
  6.5 1.0 copy-start
  6.5 3.4 %copy-start.5 = (s32[1,1,96]{2,1,0:T(1,128)S(1)}, s32[1,1,96]{2,1,0:T(1,128)}, u32[]{:S(2)}) copy-start(s32[1,1,96]{2,1,0:T(1,128)} %param.14) | copy-start | bytes 1156
  6.5 19.1 %copy-start.1 = (f32[1,1,32,64]{3,2,1,0:T(8,128)S(1)}, f32[1,1,32,64]{3,2,1,0:T(8,128)}, u32[]{:S(2)}) copy-start(f32[1,1,32,64]{3,2,1,0:T(8,128)} %param.16) | copy-start | bytes 24580
  6.5 144.8 %all-reduce.2.cloned.1.call-start = ((), (), s32[]{:S(2)}) async-start(), calls=%async_computation | async-start | bytes 393216 | tf_op jit(solution)/shard_map/psum | solution.py:71
  7.5 143.8 %copy-start.3 = (f32[64,64]{1,0:T(8,128)S(1)}, f32[64,64]{1,0:T(8,128)}, u32[]{:S(2)}) copy-start(f32[64,64]{1,0:T(8,128)} %param.17) | copy-start | bytes 49156
  7.5 145.4 %copy-start.4 = (f32[1,1,32,64]{3,2,1,0:T(8,128)S(1)}, f32[1,1,32,64]{3,2,1,0:T(8,128)}, u32[]{:S(2)}) copy-start(f32[1,1,32,64]{3,2,1,0:T(8,128)} %param.15) | copy-start | bytes 24580
  7.6 164.2 %copy-start.2 = (bf16[1,1,2048]{2,1,0:T(2,128)(2,1)S(1)}, bf16[1,1,2048]{2,1,0:T(2,128)(2,1)}, u32[]{:S(2)}) copy-start(bf16[1,1,2048]{2,1,0:T(2,128)(2,1)} %param.12) | copy-start | bytes 12292
  10.5 4.4 %collective-permute-start = (f32[3,32,384]{2,1,0:T(8,128)S(1)}, f32[3,32,384]{2,1,0:T(8,128)S(1)}, u32[]{:S(2)}, u32[]{:S(2)}) collective-permute-start(f32[3,32,384]{2,1,0:T(8,128)S(1)} %get-tuple-element.13), channel_id=1, source_target_pairs={{0,1},{2,3},{4,5},{6,7},{8,9},{10,11},{12,13},{14,15},{16,17},{18,... | collective-permute-start | bytes 442376 | tf_op jit(solution)/shard_map/ppermute | solution.py:10
  11.8 4.0 %collective-permute-start.1 = (f32[3,32,384]{2,1,0:T(8,128)S(1)}, f32[3,32,384]{2,1,0:T(8,128)S(1)}, u32[]{:S(2)}, u32[]{:S(2)}) collective-permute-start(f32[3,32,384]{2,1,0:T(8,128)S(1)} %get-tuple-element.14), channel_id=1, source_target_pairs={{1,0},{3,2},{5,4},{7,6},{9,8},{11,10},{13,12},{15,14},{17,16},{19,... | collective-permute-start | bytes 442376 | tf_op jit(solution)/shard_map/ppermute | solution.py:10
  15.8 5.3 %collective-permute-start.2 = (f32[32,384]{1,0:T(8,128)S(1)}, f32[32,384]{1,0:T(8,128)S(1)}, u32[]{:S(2)}, u32[]{:S(2)}) collective-permute-start(f32[32,384]{1,0:T(8,128)S(1)} %get-tuple-element.15), channel_id=1, source_target_pairs={{0,2},{2,4},{4,6},{6,8},{8,10},{10,12},{12,14},{14,16},{16,18},{18... | collective-permute-start | bytes 147464 | tf_op jit(solution)/shard_map/ppermute | solution.py:10
  19.0 6.6 %collective-permute-start.3 = (f32[32,384]{1,0:T(8,128)S(1)}, f32[32,384]{1,0:T(8,128)S(1)}, u32[]{:S(2)}, u32[]{:S(2)}) collective-permute-start(f32[32,384]{1,0:T(8,128)S(1)} %get-tuple-element.16), channel_id=1, source_target_pairs={{2,0},{4,2},{6,4},{8,6},{10,8},{12,10},{14,12},{16,14},{18,16},{20... | collective-permute-start | bytes 147464 | tf_op jit(solution)/shard_map/ppermute | solution.py:10
  30.1 144.4 %copy-start.6 = (bf16[1,1,2048,384]{3,2,1,0:T(8,128)(2,1)S(1)}, bf16[1,1,2048,384]{3,2,1,0:T(8,128)(2,1)}, u32[]{:S(2)}) copy-start(bf16[1,1,2048,384]{3,2,1,0:T(8,128)(2,1)} %param.9) | copy-start | bytes 4718596
  153.2 6.6 %collective-permute-start.4 = (f32[1,1,32,384]{3,2,1,0:T(8,128)S(1)}, f32[1,1,32,384]{3,2,1,0:T(8,128)S(1)}, u32[]{:S(2)}, u32[]{:S(2)}) collective-permute-start(f32[1,1,32,384]{3,2,1,0:T(8,128)S(1)} %fusion.11), channel_id=1, source_target_pairs={{0,2},{2,4},{4,6},{6,8},{8,10},{10,12},{12,14},{14,16},{16,18},{18... | collective-permute-start | bytes 147464 | tf_op jit(solution)/shard_map/ppermute | solution.py:18
  157.8 6.6 %collective-permute-start.5 = (f32[1,1,32,384]{3,2,1,0:T(8,128)S(1)}, f32[1,1,32,384]{3,2,1,0:T(8,128)S(1)}, u32[]{:S(2)}, u32[]{:S(2)}) collective-permute-start(f32[1,1,32,384]{3,2,1,0:T(8,128)S(1)} %fusion.11), channel_id=1, source_target_pairs={{2,0},{4,2},{6,4},{8,6},{10,8},{12,10},{14,12},{16,14},{18,16},{20... | collective-permute-start | bytes 147464 | tf_op jit(solution)/shard_map/ppermute | solution.py:21
  164.5 7.3 %collective-permute-start.6 = (f32[3,1,32,384]{3,2,1,0:T(8,128)S(1)}, f32[3,1,32,384]{3,2,1,0:T(8,128)S(1)}, u32[]{:S(2)}, u32[]{:S(2)}) collective-permute-start(f32[3,1,32,384]{3,2,1,0:T(8,128)S(1)} %pad_maximum_fusion.1), channel_id=1, source_target_pairs={{0,1},{2,3},{4,5},{6,7},{8,9},{10,11},{12,13},{14,15},{16,17},{18,... | collective-permute-start | bytes 442376 | tf_op jit(solution)/shard_map/ppermute | solution.py:18
  165.8 6.9 %collective-permute-start.7 = (f32[3,1,32,384]{3,2,1,0:T(8,128)S(1)}, f32[3,1,32,384]{3,2,1,0:T(8,128)S(1)}, u32[]{:S(2)}, u32[]{:S(2)}) collective-permute-start(f32[3,1,32,384]{3,2,1,0:T(8,128)S(1)} %pad_maximum_fusion.1), channel_id=1, source_target_pairs={{1,0},{3,2},{5,4},{7,6},{9,8},{11,10},{13,12},{15,14},{17,16},{19,... | collective-permute-start | bytes 442376 | tf_op jit(solution)/shard_map/ppermute | solution.py:21
  182.2 38.0 %collective-permute-start.10 = (bf16[512,384]{0,1:T(8,128)(2,1)S(1)}, bf16[512,384]{0,1:T(8,128)(2,1)S(1)}, u32[]{:S(2)}, u32[]{:S(2)}) collective-permute-start(bf16[512,384]{0,1:T(8,128)(2,1)S(1)} %get-tuple-element.11), channel_id=1, source_target_pairs={{0,1},{2,3},{4,5},{6,7},{8,9},{10,11},{12,13},{14,15},{16,17},{18,... | collective-permute-start | bytes 1179656 | tf_op jit(solution)/shard_map/ppermute | solution.py:10
  183.5 36.7 %collective-permute-start.11 = (bf16[512,384]{0,1:T(8,128)(2,1)S(1)}, bf16[512,384]{0,1:T(8,128)(2,1)S(1)}, u32[]{:S(2)}, u32[]{:S(2)}) collective-permute-start(bf16[512,384]{0,1:T(8,128)(2,1)S(1)} %get-tuple-element.10), channel_id=1, source_target_pairs={{1,0},{3,2},{5,4},{7,6},{9,8},{11,10},{13,12},{15,14},{17,16},{19,... | collective-permute-start | bytes 1179656 | tf_op jit(solution)/shard_map/ppermute | solution.py:10
  186.6 33.6 %collective-permute-start.8 = (bf16[512,384]{0,1:T(8,128)(2,1)S(1)}, bf16[512,384]{0,1:T(8,128)(2,1)S(1)}, u32[]{:S(2)}, u32[]{:S(2)}) collective-permute-start(bf16[512,384]{0,1:T(8,128)(2,1)S(1)} %get-tuple-element.9), channel_id=1, source_target_pairs={{0,2},{2,4},{4,6},{6,8},{8,10},{10,12},{12,14},{14,16},{16,18},{18... | collective-permute-start | bytes 1179656 | tf_op jit(solution)/shard_map/ppermute | solution.py:10
  188.5 31.7 %collective-permute-start.9 = (bf16[512,384]{0,1:T(8,128)(2,1)S(1)}, bf16[512,384]{0,1:T(8,128)(2,1)S(1)}, u32[]{:S(2)}, u32[]{:S(2)}) collective-permute-start(bf16[512,384]{0,1:T(8,128)(2,1)S(1)} %get-tuple-element.12), channel_id=1, source_target_pairs={{2,0},{4,2},{6,4},{8,6},{10,8},{12,10},{14,12},{16,14},{18,16},{20... | collective-permute-start | bytes 1179656 | tf_op jit(solution)/shard_map/ppermute | solution.py:10
  191.9 15.8 %collective-permute-start.12 = (bf16[512]{0:T(512)(128)(2,1)S(1)}, bf16[512]{0:T(512)(128)(2,1)S(1)}, u32[]{:S(2)}, u32[]{:S(2)}) collective-permute-start(bf16[512]{0:T(512)(128)(2,1)S(1)} %get-tuple-element.5), channel_id=1, source_target_pairs={{0,2},{2,4},{4,6},{6,8},{8,10},{10,12},{12,14},{14,16},{16,18},{18... | collective-permute-start | bytes 3080 | tf_op jit(solution)/shard_map/ppermute | solution.py:10
  207.7 6.1 %collective-permute-start.13 = (bf16[512]{0:T(512)(128)(2,1)S(1)}, bf16[512]{0:T(512)(128)(2,1)S(1)}, u32[]{:S(2)}, u32[]{:S(2)}) collective-permute-start(bf16[512]{0:T(512)(128)(2,1)S(1)} %get-tuple-element.6), channel_id=1, source_target_pairs={{2,0},{4,2},{6,4},{8,6},{10,8},{12,10},{14,12},{16,14},{18,16},{20... | collective-permute-start | bytes 3080 | tf_op jit(solution)/shard_map/ppermute | solution.py:10
  213.8 3.5 %collective-permute-start.14 = (bf16[512]{0:T(512)(128)(2,1)S(1)}, bf16[512]{0:T(512)(128)(2,1)S(1)}, u32[]{:S(2)}, u32[]{:S(2)}) collective-permute-start(bf16[512]{0:T(512)(128)(2,1)S(1)} %get-tuple-element.8), channel_id=1, source_target_pairs={{0,1},{2,3},{4,5},{6,7},{8,9},{10,11},{12,13},{14,15},{16,17},{18,... | collective-permute-start | bytes 3080 | tf_op jit(solution)/shard_map/ppermute | solution.py:10
  217.3 2.9 %collective-permute-start.15 = (bf16[512]{0:T(512)(128)(2,1)S(1)}, bf16[512]{0:T(512)(128)(2,1)S(1)}, u32[]{:S(2)}, u32[]{:S(2)}) collective-permute-start(bf16[512]{0:T(512)(128)(2,1)S(1)} %get-tuple-element.7), channel_id=1, source_target_pairs={{1,0},{3,2},{5,4},{7,6},{9,8},{11,10},{13,12},{15,14},{17,16},{19,... | collective-permute-start | bytes 3080 | tf_op jit(solution)/shard_map/ppermute | solution.py:10
Sparse Core Ops, SparseCore 0:
  26.9 124.3 all-reduce.1
where the time goes:
time: 230 us; the launch traced here: 229 us
  waiting for transfers between devices  152 us (66%)
  starting transfers between devices  42 us (18%)
  matrix products  15.1 us (7%)
  between operations  13.8 us (6%)
  blocking collectives  3.32 us (1%)
    psum x1, waiting for transfers between devices, local(): lax.psum(jnp.einsum('cl,cr->lr', level_phi, assembled, precision=highest)...  121 us
    ppermute x12, starting transfers between devices, passed_along(): return lax.ppermute(block, axis, route)  28.2 us
    ppermute x12, waiting for transfers between devices, passed_along(): return lax.ppermute(block, axis, route)  24.7 us
    ppermute x2, starting transfers between devices, extended(): lax.ppermute(lax.slice_in_dim(block, 0, width, axis=dim), axis, backward)  7.86 us
    dot_general x1, matrix products, local(): jnp.dot(local_inverse[0, 0], masked, preferred_element_type=jnp.float32)  7.52 us
    ppermute x2, starting transfers between devices, extended(): lax.ppermute(lax.slice_in_dim(block, block.shape[dim] - width, None, axis...  5.93 us
    ppermute x2, waiting for transfers between devices, extended(): lax.ppermute(lax.slice_in_dim(block, 0, width, axis=dim), axis, backward)  5.64 us
  transfers between devices with their start and end apart: 17, of which 9 were waited for; matrix products, arithmetic and copies ran while one was open for 0% of the time, Pallas kernels for 0%

commit v1 on v0

--- a/solution.py
+++ b/solution.py
@@ -1,7 +1,16 @@
+import functools
 import jax
 import jax.numpy as jnp
 from jax import lax
 from jax.sharding import PartitionSpec as P
+
+
+def treat_plate_by_axis(u_in, mesh_ax):
+    local_out = lax.all_gather(u_in, mesh_ax)
+    return jnp.sum(local_out, axis=0)
+
+
+islands_process = functools.partial(treat_plate_by_axis, mesh_ax=("gx", "gy"))
 
 
 def passed_along(block, axis, distance):
@@ -68,9 +77,7 @@
     from_above_x = passed_along(along_x[0], "gx", -1)
     assembled = along_x[1] + from_below_x + from_above_x
     level_phi = level_basis[0, 0]
-    top_rhs = lax.psum(
-        jnp.einsum("cl,cr->lr", level_phi, assembled, precision=highest), ("gx", "gy")
-    )
+    top_rhs = islands_process(jnp.einsum("cl,cr->lr", level_phi, assembled, precision=highest))
     top_value = jnp.dot(top_inverse, top_rhs, precision=highest)
     block_rhs = lax.all_gather(assembled, "gy", axis=0, tiled=True)
     coarse = jnp.dot(block_inverse[0, 0], block_rhs, precision=highest) + jnp.dot(

time: 230 us -> 162 us (0.70)
  waiting for transfers between devices: 152 us -> 86.5 us
  starting transfers between devices: 42 us -> 38.4 us
    psum x1 -> x0, waiting for transfers between devices: 121 us -> none  [local(): lax.psum(jnp.einsum('cl,cr->lr', level_phi, assembled, precision=highest)...]
    all_gather x0 -> x1, waiting for transfers between devices: none -> 56.7 us  [treat_plate_by_axis(): local_out = lax.all_gather(u_in, mesh_ax)]
where the time goes in v1:
time: 162 us
  waiting for transfers between devices  86.5 us (53%)
  starting transfers between devices  38.4 us (24%)
  matrix products  14.1 us (9%)
  between operations  13.8 us (9%)
  other arithmetic  3.59 us (2%)
  blocking collectives  3.32 us (2%)
  local copies, waits for them, and re-layouts  1.97 us (1%)
    all_gather x1, waiting for transfers between devices, treat_plate_by_axis(): local_out = lax.all_gather(u_in, mesh_ax)  56.7 us
    ppermute x12, starting transfers between devices, passed_along(): return lax.ppermute(block, axis, route)  28.2 us
    ppermute x12, waiting for transfers between devices, passed_along(): return lax.ppermute(block, axis, route)  24.7 us
    dot_general x1, matrix products, local(): jnp.dot(local_inverse[0, 0], masked, preferred_element_type=jnp.float32)  7.52 us
    ppermute x2, starting transfers between devices, extended(): lax.ppermute(lax.slice_in_dim(block, 0, width, axis=dim), axis, backward)  6.03 us
    ppermute x2, waiting for transfers between devices, extended(): lax.ppermute(lax.slice_in_dim(block, 0, width, axis=dim), axis, backward)  5.14 us
    ppermute x2, starting transfers between devices, extended(): lax.ppermute(lax.slice_in_dim(block, block.shape[dim] - width, None, axis...  4.16 us
    all_gather x1, blocking collectives, local(): block_rhs = lax.all_gather(assembled, 'gy', axis=0, tiled=True)  3.32 us
  transfers between devices with their start and end apart: 17, of which 9 were waited for; matrix products, arithmetic and copies ran while one was open for 0% of the time, Pallas kernels for 0%

profile of v1, /device:TPU:7, one launch (start us, length us, event | category | flops | bytes accessed | tf_op | source)
XLA Modules:
  0.0 161.7 jit_solution(5696783777811926736)
XLA Ops:
  6.5 0.0 copy-start
  6.5 0.0 copy-start.5
  6.5 0.0 copy-start.1
  6.5 0.0 all-gather.3.cloned.1.call-start
  6.6 0.8 select_reduce_fusion
  7.4 0.2 copy-done
  7.5 2.4 %fusion.7 = f32[384,96]{1,0:T(8,128)S(1)} fusion(bf16[1,1,2048,384]{3,2,1,0:T(8,128)(2,1)} %param.9, pred[2048]{0:T(1024)(128)(4,1)S(1)} %fusion.29, bf16[1,1,96,2048]{3,2,1,0:T(8,128)(2,1)S(1)} %copy-done), kind=kOutput, calls=%fused_computation.5 | convolution fusion | flops 151781376 | bytes 2115584 | tf_op jit(solution)/shard_map/dot_general | solution.py:66
  9.9 0.0 copy-start.2
  9.9 0.0 copy-done.5
  10.0 0.0 copy-start.4
  10.0 0.5 fusion.19
  10.4 0.0 copy-start.3
  10.5 1.3 collective-permute-start
  11.8 3.0 %collective-permute-start.1 = (f32[3,32,384]{2,1,0:T(8,128)S(1)}, f32[3,32,384]{2,1,0:T(8,128)S(1)}, u32[]{:S(2)}, u32[]{:S(2)}) collective-permute-start(f32[3,32,384]{2,1,0:T(8,128)S(1)} %get-tuple-element.14), channel_id=1, source_target_pairs={{1,0},{3,2},{5,4},{7,6},{9,8},{11,10},{13,12},{15,14},{17,16},{19,... | collective-permute-start | bytes 442376 | tf_op jit(solution)/shard_map/ppermute | solution.py:19
  14.8 0.0 collective-permute-done
  14.8 1.0 collective-permute-done.1
  15.8 3.1 %collective-permute-start.2 = (f32[32,384]{1,0:T(8,128)S(1)}, f32[32,384]{1,0:T(8,128)S(1)}, u32[]{:S(2)}, u32[]{:S(2)}) collective-permute-start(f32[32,384]{1,0:T(8,128)S(1)} %get-tuple-element.15), channel_id=1, source_target_pairs={{0,2},{2,4},{4,6},{6,8},{8,10},{10,12},{12,14},{14,16},{16,18},{18... | collective-permute-start | bytes 147464 | tf_op jit(solution)/shard_map/ppermute | solution.py:19
  19.0 2.2 %collective-permute-start.3 = (f32[32,384]{1,0:T(8,128)S(1)}, f32[32,384]{1,0:T(8,128)S(1)}, u32[]{:S(2)}, u32[]{:S(2)}) collective-permute-start(f32[32,384]{1,0:T(8,128)S(1)} %get-tuple-element.16), channel_id=1, source_target_pairs={{2,0},{4,2},{6,4},{8,6},{10,8},{12,10},{14,12},{16,14},{18,16},{20... | collective-permute-start | bytes 147464 | tf_op jit(solution)/shard_map/ppermute | solution.py:19
  21.1 0.0 collective-permute-done.2
  21.2 4.5 %collective-permute-done.3 = f32[32,384]{1,0:T(8,128)S(1)} collective-permute-done((f32[32,384]{1,0:T(8,128)S(1)}, f32[32,384]{1,0:T(8,128)S(1)}, u32[]{:S(2)}, u32[]{:S(2)}) %collective-permute-start.3) | collective-permute-done | bytes 49184 | tf_op jit(solution)/shard_map/ppermute | solution.py:19
  25.6 0.0 copy-done.1
  25.6 0.9 convolution_bitcast_fusion
  26.6 0.0 all-gather.3.cloned.1.call-update
  26.6 3.3 %all_gather.9 = f32[64,384]{1,0:T(8,128)S(1)} all-gather(f32[32,384]{1,0:T(8,128)S(1)} %fusion.24), channel_id=1, replica_groups=mesh['gx'=16,'gy'=2] {'gy'}, dimensions={0}, use_global_device_ids=true | all-gather | bytes 147456 | tf_op jit(solution)/shard_map/all_gather | solution.py:82
  29.9 56.7 %all-gather.3.cloned.1.call-done = f32[2048,384]{1,0:T(8,128)} async-done(((f32[64,384]{1,0:T(8,128)}), f32[2048,384]{1,0:T(8,128)}) %all-gather.3.cloned.1.call-update) | async-done | bytes 3145744 | tf_op jit(solution)/shard_map/all_gather | solution.py:9
  86.6 2.0 %reduce_sum.19 = f32[64,384]{1,0:T(8,128)S(1)} reduce(f32[32,64,384]{2,1,0:T(8,128)} %bitcast.73, f32[]{:T(128)} %constant.35.clone.1), dimensions={0}, to_apply=%region_1.2 | reduce | flops 761856 | bytes 3244036 | tf_op jit(solution)/shard_map/reduce_sum | solution.py:10
  88.7 0.0 copy-done.2
  88.7 0.0 copy-start.6
  88.7 0.5 fusion.38
  89.2 0.3 fusion.25
  89.5 0.0 copy-done.4
  89.5 0.2 fusion.11
  89.7 2.9 %collective-permute-start.4 = (f32[1,1,32,384]{3,2,1,0:T(8,128)S(1)}, f32[1,1,32,384]{3,2,1,0:T(8,128)S(1)}, u32[]{:S(2)}, u32[]{:S(2)}) collective-permute-start(f32[1,1,32,384]{3,2,1,0:T(8,128)S(1)} %fusion.11), channel_id=1, source_target_pairs={{0,2},{2,4},{4,6},{6,8},{8,10},{10,12},{12,14},{14,16},{16,18},{18... | collective-permute-start | bytes 147464 | tf_op jit(solution)/shard_map/ppermute | solution.py:27
  92.6 2.4 %collective-permute-start.5 = (f32[1,1,32,384]{3,2,1,0:T(8,128)S(1)}, f32[1,1,32,384]{3,2,1,0:T(8,128)S(1)}, u32[]{:S(2)}, u32[]{:S(2)}) collective-permute-start(f32[1,1,32,384]{3,2,1,0:T(8,128)S(1)} %fusion.11), channel_id=1, source_target_pairs={{2,0},{4,2},{6,4},{8,6},{10,8},{12,10},{14,12},{16,14},{18,16},{20... | collective-permute-start | bytes 147464 | tf_op jit(solution)/shard_map/ppermute | solution.py:30
  95.0 0.0 collective-permute-done.4
  95.0 4.2 %collective-permute-done.5 = f32[1,1,32,384]{3,2,1,0:T(8,128)S(1)} collective-permute-done((f32[1,1,32,384]{3,2,1,0:T(8,128)S(1)}, f32[1,1,32,384]{3,2,1,0:T(8,128)S(1)}, u32[]{:S(2)}, u32[]{:S(2)}) %collective-permute-start.5) | collective-permute-done | bytes 49184 | tf_op jit(solution)/shard_map/ppermute | solution.py:30
  99.3 1.3 collective-permute-start.6
  100.6 3.6 %collective-permute-start.7 = (f32[3,1,32,384]{3,2,1,0:T(8,128)S(1)}, f32[3,1,32,384]{3,2,1,0:T(8,128)S(1)}, u32[]{:S(2)}, u32[]{:S(2)}) collective-permute-start(f32[3,1,32,384]{3,2,1,0:T(8,128)S(1)} %pad_maximum_fusion.1), channel_id=1, source_target_pairs={{1,0},{3,2},{5,4},{7,6},{9,8},{11,10},{13,12},{15,14},{17,16},{19,... | collective-permute-start | bytes 442376 | tf_op jit(solution)/shard_map/ppermute | solution.py:30
  104.2 0.0 copy-done.3
  104.2 0.0 collective-permute-done.6
  104.2 0.9 collective-permute-done.7
  105.2 0.4 fusion.17
  105.6 1.4 fusion.12
  107.0 0.0 copy-done.6
  107.0 7.5 %fusion.4 = bf16[2048,384]{0,1:T(8,128)(2,1)S(1)} fusion(f32[384,2048]{1,0:T(8,128)S(1)} %fusion.12, bf16[1,1,2048,2048]{3,2,1,0:T(8,128)(2,1)} %param.10, f32[2048]{0:T(1024)S(1)} %bitcast.77, pred[2048]{0:T(1024)(128)(4,1)S(1)} %fusion.29, bf16[1,1,2048,384]{3,2,1,0:T(8,128)(2,1)S(1)} %copy-done.6), kind=kOutput, calls=%fused_computation.4 | convolution fusion | flops 3226730496 | bytes 14690304 | tf_op jit(solution)/shard_map/dot_general | solution.py:64
  114.6 0.1 fusion.37
  114.7 1.3 collective-permute-start.10
  116.0 3.1 %collective-permute-start.11 = (bf16[512,384]{0,1:T(8,128)(2,1)S(1)}, bf16[512,384]{0,1:T(8,128)(2,1)S(1)}, u32[]{:S(2)}, u32[]{:S(2)}) collective-permute-start(bf16[512,384]{0,1:T(8,128)(2,1)S(1)} %get-tuple-element.10), channel_id=1, source_target_pairs={{1,0},{3,2},{5,4},{7,6},{9,8},{11,10},{13,12},{15,14},{17,16},{19,... | collective-permute-start | bytes 1179656 | tf_op jit(solution)/shard_map/ppermute | solution.py:19
  119.1 1.9 %collective-permute-start.8 = (bf16[512,384]{0,1:T(8,128)(2,1)S(1)}, bf16[512,384]{0,1:T(8,128)(2,1)S(1)}, u32[]{:S(2)}, u32[]{:S(2)}) collective-permute-start(bf16[512,384]{0,1:T(8,128)(2,1)S(1)} %get-tuple-element.9), channel_id=1, source_target_pairs={{0,2},{2,4},{4,6},{6,8},{8,10},{10,12},{12,14},{14,16},{16,18},{18... | collective-permute-start | bytes 1179656 | tf_op jit(solution)/shard_map/ppermute | solution.py:19
  121.0 3.4 %collective-permute-start.9 = (bf16[512,384]{0,1:T(8,128)(2,1)S(1)}, bf16[512,384]{0,1:T(8,128)(2,1)S(1)}, u32[]{:S(2)}, u32[]{:S(2)}) collective-permute-start(bf16[512,384]{0,1:T(8,128)(2,1)S(1)} %get-tuple-element.12), channel_id=1, source_target_pairs={{2,0},{4,2},{6,4},{8,6},{10,8},{12,10},{14,12},{16,14},{18,16},{20... | collective-permute-start | bytes 1179656 | tf_op jit(solution)/shard_map/ppermute | solution.py:19
  124.4 3.7 %collective-permute-start.12 = (bf16[512]{0:T(512)(128)(2,1)S(1)}, bf16[512]{0:T(512)(128)(2,1)S(1)}, u32[]{:S(2)}, u32[]{:S(2)}) collective-permute-start(bf16[512]{0:T(512)(128)(2,1)S(1)} %get-tuple-element.5), channel_id=1, source_target_pairs={{0,2},{2,4},{4,6},{6,8},{8,10},{10,12},{12,14},{14,16},{16,18},{18... | collective-permute-start | bytes 3080 | tf_op jit(solution)/shard_map/ppermute | solution.py:19
  128.1 12.1 %collective-permute-done.12 = bf16[512]{0:T(512)(128)(2,1)S(1)} collective-permute-done((bf16[512]{0:T(512)(128)(2,1)S(1)}, bf16[512]{0:T(512)(128)(2,1)S(1)}, u32[]{:S(2)}, u32[]{:S(2)}) %collective-permute-start.12) | collective-permute-done | bytes 1056 | tf_op jit(solution)/shard_map/ppermute | solution.py:19
  140.2 1.9 %collective-permute-start.13 = (bf16[512]{0:T(512)(128)(2,1)S(1)}, bf16[512]{0:T(512)(128)(2,1)S(1)}, u32[]{:S(2)}, u32[]{:S(2)}) collective-permute-start(bf16[512]{0:T(512)(128)(2,1)S(1)} %get-tuple-element.6), channel_id=1, source_target_pairs={{2,0},{4,2},{6,4},{8,6},{10,8},{12,10},{14,12},{16,14},{18,16},{20... | collective-permute-start | bytes 3080 | tf_op jit(solution)/shard_map/ppermute | solution.py:19
  142.1 4.2 %collective-permute-done.13 = bf16[512]{0:T(512)(128)(2,1)S(1)} collective-permute-done((bf16[512]{0:T(512)(128)(2,1)S(1)}, bf16[512]{0:T(512)(128)(2,1)S(1)}, u32[]{:S(2)}, u32[]{:S(2)}) %collective-permute-start.13) | collective-permute-done | bytes 1056 | tf_op jit(solution)/shard_map/ppermute | solution.py:19
  146.3 1.3 collective-permute-start.14
  147.6 2.2 %collective-permute-done.14 = bf16[512]{0:T(512)(128)(2,1)S(1)} collective-permute-done((bf16[512]{0:T(512)(128)(2,1)S(1)}, bf16[512]{0:T(512)(128)(2,1)S(1)}, u32[]{:S(2)}, u32[]{:S(2)}) %collective-permute-start.14) | collective-permute-done | bytes 1056 | tf_op jit(solution)/shard_map/ppermute | solution.py:19
  149.8 2.1 %collective-permute-start.15 = (bf16[512]{0:T(512)(128)(2,1)S(1)}, bf16[512]{0:T(512)(128)(2,1)S(1)}, u32[]{:S(2)}, u32[]{:S(2)}) collective-permute-start(bf16[512]{0:T(512)(128)(2,1)S(1)} %get-tuple-element.7), channel_id=1, source_target_pairs={{1,0},{3,2},{5,4},{7,6},{9,8},{11,10},{13,12},{15,14},{17,16},{19,... | collective-permute-start | bytes 3080 | tf_op jit(solution)/shard_map/ppermute | solution.py:19
  151.8 0.8 collective-permute-done.15
  152.6 0.0 collective-permute-done.10
  152.6 0.0 collective-permute-done.11
  152.7 0.0 collective-permute-done.8
  152.7 0.0 collective-permute-done.9
  152.7 0.6 fusion.10
  153.3 1.6 copy.15
  (11 shorter events, 0.2 us)
Async XLA Ops:
  6.5 1.0 copy-start
  6.5 3.4 %copy-start.5 = (s32[1,1,96]{2,1,0:T(1,128)S(1)}, s32[1,1,96]{2,1,0:T(1,128)}, u32[]{:S(2)}) copy-start(s32[1,1,96]{2,1,0:T(1,128)} %param.14) | copy-start | bytes 1156
  6.5 19.1 %copy-start.1 = (f32[1,1,32,64]{3,2,1,0:T(8,128)S(1)}, f32[1,1,32,64]{3,2,1,0:T(8,128)}, u32[]{:S(2)}) copy-start(f32[1,1,32,64]{3,2,1,0:T(8,128)} %param.16) | copy-start | bytes 24580
  6.5 80.1 %all-gather.3.cloned.1.call-start = ((), (), s32[]{:S(2)}) async-start(), calls=%async_computation | async-start | bytes 3244032 | tf_op jit(solution)/shard_map/all_gather | solution.py:9
  9.9 78.7 %copy-start.2 = (f32[64,64]{1,0:T(8,128)S(1)}, f32[64,64]{1,0:T(8,128)}, u32[]{:S(2)}) copy-start(f32[64,64]{1,0:T(8,128)} %param.17) | copy-start | bytes 49156
  10.0 79.6 %copy-start.4 = (f32[1,1,32,64]{3,2,1,0:T(8,128)S(1)}, f32[1,1,32,64]{3,2,1,0:T(8,128)}, u32[]{:S(2)}) copy-start(f32[1,1,32,64]{3,2,1,0:T(8,128)} %param.15) | copy-start | bytes 24580
  10.4 93.8 %copy-start.3 = (bf16[1,1,2048]{2,1,0:T(2,128)(2,1)S(1)}, bf16[1,1,2048]{2,1,0:T(2,128)(2,1)}, u32[]{:S(2)}) copy-start(bf16[1,1,2048]{2,1,0:T(2,128)(2,1)} %param.12) | copy-start | bytes 12292
  10.5 4.4 %collective-permute-start = (f32[3,32,384]{2,1,0:T(8,128)S(1)}, f32[3,32,384]{2,1,0:T(8,128)S(1)}, u32[]{:S(2)}, u32[]{:S(2)}) collective-permute-start(f32[3,32,384]{2,1,0:T(8,128)S(1)} %get-tuple-element.13), channel_id=1, source_target_pairs={{0,1},{2,3},{4,5},{6,7},{8,9},{10,11},{12,13},{14,15},{16,17},{18,... | collective-permute-start | bytes 442376 | tf_op jit(solution)/shard_map/ppermute | solution.py:19
  11.8 4.0 %collective-permute-start.1 = (f32[3,32,384]{2,1,0:T(8,128)S(1)}, f32[3,32,384]{2,1,0:T(8,128)S(1)}, u32[]{:S(2)}, u32[]{:S(2)}) collective-permute-start(f32[3,32,384]{2,1,0:T(8,128)S(1)} %get-tuple-element.14), channel_id=1, source_target_pairs={{1,0},{3,2},{5,4},{7,6},{9,8},{11,10},{13,12},{15,14},{17,16},{19,... | collective-permute-start | bytes 442376 | tf_op jit(solution)/shard_map/ppermute | solution.py:19
  15.8 5.3 %collective-permute-start.2 = (f32[32,384]{1,0:T(8,128)S(1)}, f32[32,384]{1,0:T(8,128)S(1)}, u32[]{:S(2)}, u32[]{:S(2)}) collective-permute-start(f32[32,384]{1,0:T(8,128)S(1)} %get-tuple-element.15), channel_id=1, source_target_pairs={{0,2},{2,4},{4,6},{6,8},{8,10},{10,12},{12,14},{14,16},{16,18},{18... | collective-permute-start | bytes 147464 | tf_op jit(solution)/shard_map/ppermute | solution.py:19
  19.0 6.6 %collective-permute-start.3 = (f32[32,384]{1,0:T(8,128)S(1)}, f32[32,384]{1,0:T(8,128)S(1)}, u32[]{:S(2)}, u32[]{:S(2)}) collective-permute-start(f32[32,384]{1,0:T(8,128)S(1)} %get-tuple-element.16), channel_id=1, source_target_pairs={{2,0},{4,2},{6,4},{8,6},{10,8},{12,10},{14,12},{16,14},{18,16},{20... | collective-permute-start | bytes 147464 | tf_op jit(solution)/shard_map/ppermute | solution.py:19
  88.7 18.4 %copy-start.6 = (bf16[1,1,2048,384]{3,2,1,0:T(8,128)(2,1)S(1)}, bf16[1,1,2048,384]{3,2,1,0:T(8,128)(2,1)}, u32[]{:S(2)}) copy-start(bf16[1,1,2048,384]{3,2,1,0:T(8,128)(2,1)} %param.9) | copy-start | bytes 4718596
  89.7 5.3 %collective-permute-start.4 = (f32[1,1,32,384]{3,2,1,0:T(8,128)S(1)}, f32[1,1,32,384]{3,2,1,0:T(8,128)S(1)}, u32[]{:S(2)}, u32[]{:S(2)}) collective-permute-start(f32[1,1,32,384]{3,2,1,0:T(8,128)S(1)} %fusion.11), channel_id=1, source_target_pairs={{0,2},{2,4},{4,6},{6,8},{8,10},{10,12},{12,14},{14,16},{16,18},{18... | collective-permute-start | bytes 147464 | tf_op jit(solution)/shard_map/ppermute | solution.py:27
  92.6 6.6 %collective-permute-start.5 = (f32[1,1,32,384]{3,2,1,0:T(8,128)S(1)}, f32[1,1,32,384]{3,2,1,0:T(8,128)S(1)}, u32[]{:S(2)}, u32[]{:S(2)}) collective-permute-start(f32[1,1,32,384]{3,2,1,0:T(8,128)S(1)} %fusion.11), channel_id=1, source_target_pairs={{2,0},{4,2},{6,4},{8,6},{10,8},{12,10},{14,12},{16,14},{18,16},{20... | collective-permute-start | bytes 147464 | tf_op jit(solution)/shard_map/ppermute | solution.py:30
  99.3 5.0 %collective-permute-start.6 = (f32[3,1,32,384]{3,2,1,0:T(8,128)S(1)}, f32[3,1,32,384]{3,2,1,0:T(8,128)S(1)}, u32[]{:S(2)}, u32[]{:S(2)}) collective-permute-start(f32[3,1,32,384]{3,2,1,0:T(8,128)S(1)} %pad_maximum_fusion.1), channel_id=1, source_target_pairs={{0,1},{2,3},{4,5},{6,7},{8,9},{10,11},{12,13},{14,15},{16,17},{18,... | collective-permute-start | bytes 442376 | tf_op jit(solution)/shard_map/ppermute | solution.py:27
  100.6 4.6 %collective-permute-start.7 = (f32[3,1,32,384]{3,2,1,0:T(8,128)S(1)}, f32[3,1,32,384]{3,2,1,0:T(8,128)S(1)}, u32[]{:S(2)}, u32[]{:S(2)}) collective-permute-start(f32[3,1,32,384]{3,2,1,0:T(8,128)S(1)} %pad_maximum_fusion.1), channel_id=1, source_target_pairs={{1,0},{3,2},{5,4},{7,6},{9,8},{11,10},{13,12},{15,14},{17,16},{19,... | collective-permute-start | bytes 442376 | tf_op jit(solution)/shard_map/ppermute | solution.py:30
  114.7 38.0 %collective-permute-start.10 = (bf16[512,384]{0,1:T(8,128)(2,1)S(1)}, bf16[512,384]{0,1:T(8,128)(2,1)S(1)}, u32[]{:S(2)}, u32[]{:S(2)}) collective-permute-start(bf16[512,384]{0,1:T(8,128)(2,1)S(1)} %get-tuple-element.11), channel_id=1, source_target_pairs={{0,1},{2,3},{4,5},{6,7},{8,9},{10,11},{12,13},{14,15},{16,17},{18,... | collective-permute-start | bytes 1179656 | tf_op jit(solution)/shard_map/ppermute | solution.py:19
  116.0 36.7 %collective-permute-start.11 = (bf16[512,384]{0,1:T(8,128)(2,1)S(1)}, bf16[512,384]{0,1:T(8,128)(2,1)S(1)}, u32[]{:S(2)}, u32[]{:S(2)}) collective-permute-start(bf16[512,384]{0,1:T(8,128)(2,1)S(1)} %get-tuple-element.10), channel_id=1, source_target_pairs={{1,0},{3,2},{5,4},{7,6},{9,8},{11,10},{13,12},{15,14},{17,16},{19,... | collective-permute-start | bytes 1179656 | tf_op jit(solution)/shard_map/ppermute | solution.py:19
  119.1 33.6 %collective-permute-start.8 = (bf16[512,384]{0,1:T(8,128)(2,1)S(1)}, bf16[512,384]{0,1:T(8,128)(2,1)S(1)}, u32[]{:S(2)}, u32[]{:S(2)}) collective-permute-start(bf16[512,384]{0,1:T(8,128)(2,1)S(1)} %get-tuple-element.9), channel_id=1, source_target_pairs={{0,2},{2,4},{4,6},{6,8},{8,10},{10,12},{12,14},{14,16},{16,18},{18... | collective-permute-start | bytes 1179656 | tf_op jit(solution)/shard_map/ppermute | solution.py:19
  121.0 31.7 %collective-permute-start.9 = (bf16[512,384]{0,1:T(8,128)(2,1)S(1)}, bf16[512,384]{0,1:T(8,128)(2,1)S(1)}, u32[]{:S(2)}, u32[]{:S(2)}) collective-permute-start(bf16[512,384]{0,1:T(8,128)(2,1)S(1)} %get-tuple-element.12), channel_id=1, source_target_pairs={{2,0},{4,2},{6,4},{8,6},{10,8},{12,10},{14,12},{16,14},{18,16},{20... | collective-permute-start | bytes 1179656 | tf_op jit(solution)/shard_map/ppermute | solution.py:19
  124.4 15.8 %collective-permute-start.12 = (bf16[512]{0:T(512)(128)(2,1)S(1)}, bf16[512]{0:T(512)(128)(2,1)S(1)}, u32[]{:S(2)}, u32[]{:S(2)}) collective-permute-start(bf16[512]{0:T(512)(128)(2,1)S(1)} %get-tuple-element.5), channel_id=1, source_target_pairs={{0,2},{2,4},{4,6},{6,8},{8,10},{10,12},{12,14},{14,16},{16,18},{18... | collective-permute-start | bytes 3080 | tf_op jit(solution)/shard_map/ppermute | solution.py:19
  140.2 6.1 %collective-permute-start.13 = (bf16[512]{0:T(512)(128)(2,1)S(1)}, bf16[512]{0:T(512)(128)(2,1)S(1)}, u32[]{:S(2)}, u32[]{:S(2)}) collective-permute-start(bf16[512]{0:T(512)(128)(2,1)S(1)} %get-tuple-element.6), channel_id=1, source_target_pairs={{2,0},{4,2},{6,4},{8,6},{10,8},{12,10},{14,12},{16,14},{18,16},{20... | collective-permute-start | bytes 3080 | tf_op jit(solution)/shard_map/ppermute | solution.py:19
  146.3 3.5 %collective-permute-start.14 = (bf16[512]{0:T(512)(128)(2,1)S(1)}, bf16[512]{0:T(512)(128)(2,1)S(1)}, u32[]{:S(2)}, u32[]{:S(2)}) collective-permute-start(bf16[512]{0:T(512)(128)(2,1)S(1)} %get-tuple-element.8), channel_id=1, source_target_pairs={{0,1},{2,3},{4,5},{6,7},{8,9},{10,11},{12,13},{14,15},{16,17},{18,... | collective-permute-start | bytes 3080 | tf_op jit(solution)/shard_map/ppermute | solution.py:19
  149.8 2.9 %collective-permute-start.15 = (bf16[512]{0:T(512)(128)(2,1)S(1)}, bf16[512]{0:T(512)(128)(2,1)S(1)}, u32[]{:S(2)}, u32[]{:S(2)}) collective-permute-start(bf16[512]{0:T(512)(128)(2,1)S(1)} %get-tuple-element.7), channel_id=1, source_target_pairs={{1,0},{3,2},{5,4},{7,6},{9,8},{11,10},{13,12},{15,14},{17,16},{19,... | collective-permute-start | bytes 3080 | tf_op jit(solution)/shard_map/ppermute | solution.py:19
Sparse Core Ops, SparseCore 0:
  26.7 59.8 all-gather.2
